TPU v7x, 32 devices: a whole 2x2x4 slice. The times are simulated.
32 devices in a mesh: atoms: 8 (over y, x, core), gsplit: 4 (over z).
Axes of the slice: x: 2, y: 2, z: 4, core: 2. Of those that a mesh axis runs over, the one named last changes fastest.
Arguments:
- miller: int32 [3, 30720], P(None, 'gsplit'), may hold values from -16 to 16, as said below
- form_factors: bfloat16 [49, 30720], P(None, 'gsplit'), may hold values from -6 to 6
- fractional: float32 [3, 512], P(None, 'atoms'), may hold values from 0 to 1
- multipoles: bfloat16 [2, 49, 512], P(None, None, 'atoms'), may hold values from -0.0390625 to 0.0390625
- point_owner: int32 [1024], P(('atoms', 'gsplit')), may hold values from 0 to 63
- offsets: float32 [3, 1024], P(None, ('atoms', 'gsplit')), may hold values from -0.05 to 0.05
Outputs:
- grid_potential: float32 [2, 1024], P(None, ('atoms', 'gsplit'))
- moments: float32 [2, 49, 512], P(None, None, ('atoms', 'gsplit'))
Inputs may be any that keep to these rules, and one draw needn't show every extreme that they name: `miller`: no vector has all three indices zero. Point p belongs to atom (p // 128) * 64 + point_owner[p].
All inputs are finite; a program needn't handle non-finite values.
Results may differ from a plain program's by a relative error of at most 0.0045.
Values may be sent and summed in bfloat16 or wider, within the bound.
A program may use at most 64 MiB of HBM per device.

v0:
```python
import math
import jax
import jax.numpy as jnp
from jax import lax
from jax.sharding import PartitionSpec as P

two_pi = 2.0 * math.pi
damping = 1.0 / 400.0


def angles(vectors, places):
    indices = vectors.astype(jnp.float32)
    summed = (
        places[0][:, None] * indices[0][None, :]
        + places[1][:, None] * indices[1][None, :]
        + places[2][:, None] * indices[2][None, :]
    )
    return two_pi * summed


def sign_tables(comp_count):
    comp_ids = jnp.arange(comp_count, dtype=jnp.int32)
    degree = jnp.zeros((comp_count,), jnp.int32)
    for degree_step in range(1, 16):
        degree = degree + (comp_ids >= degree_step * degree_step).astype(jnp.int32)
    quarter = degree % 4
    even_sign = jnp.where(quarter == 0, 1.0, jnp.where(quarter == 2, -1.0, 0.0)).astype(jnp.float32)
    odd_sign = jnp.where(quarter == 3, 1.0, jnp.where(quarter == 1, -1.0, 0.0)).astype(jnp.float32)
    return (even_sign, odd_sign)


def coulomb(vectors):
    indices = vectors.astype(jnp.float32)
    square = indices[0] * indices[0] + indices[1] * indices[1] + indices[2] * indices[2]
    return jnp.exp(-damping * square) / square


def structure(multipoles, cos_table, sin_table, form_block, even_sign, odd_sign):
    density_count, comp_count, atom_count = multipoles.shape
    flattened = multipoles.reshape(density_count * comp_count, atom_count)
    along_cos = jnp.dot(flattened, cos_table, preferred_element_type=jnp.float32).reshape(
        density_count, comp_count, -1
    )
    along_sin = jnp.dot(flattened, sin_table, preferred_element_type=jnp.float32).reshape(
        density_count, comp_count, -1
    )
    weights = form_block.astype(jnp.float32)[None]
    even_wide = even_sign[None, :, None]
    odd_wide = odd_sign[None, :, None]
    real_part = jnp.sum(weights * (even_wide * along_cos + odd_wide * along_sin), axis=1)
    imag_part = jnp.sum(weights * (odd_wide * along_cos - even_wide * along_sin), axis=1)
    return jnp.stack([real_part, imag_part], axis=1)


def moment_terms(potential, form_block, cos_table, sin_table, even_sign, odd_sign):
    weighted = (form_block.astype(jnp.float32)[None, None] * potential[:, :, None, :]).astype(
        jnp.bfloat16
    )
    density_count, _, comp_count, vector_count = weighted.shape
    even_rows = (even_sign != 0.0)[None, :, None]
    against_cos = jnp.where(even_rows, weighted[:, 0], weighted[:, 1]).reshape(
        density_count * comp_count, vector_count
    )
    against_sin = jnp.where(even_rows, weighted[:, 1], weighted[:, 0]).reshape(
        density_count * comp_count, vector_count
    )
    contract = (((1,), (1,)), ((), ()))
    with_cos = lax.dot_general(
        against_cos, cos_table, contract, preferred_element_type=jnp.float32
    ).reshape(density_count, comp_count, -1)
    with_sin = lax.dot_general(
        against_sin, sin_table, contract, preferred_element_type=jnp.float32
    ).reshape(density_count, comp_count, -1)
    even_wide = even_sign[None, :, None]
    odd_wide = odd_sign[None, :, None]
    return even_wide * (with_cos - with_sin) + odd_wide * (with_cos + with_sin)


def grid_rows(rounded, vectors, places):
    point_angles = angles(vectors, places)
    cos_points = jnp.cos(point_angles).astype(jnp.bfloat16)
    sin_points = jnp.sin(point_angles).astype(jnp.bfloat16)
    contract = (((1,), (1,)), ((), ()))
    return lax.dot_general(
        cos_points, rounded[:, 0], contract, preferred_element_type=jnp.float32
    ) - lax.dot_general(sin_points, rounded[:, 1], contract, preferred_element_type=jnp.float32)


def grid_blocked(rounded, vectors, places):
    point_count = places.shape[1]
    return grid_rows(rounded, vectors, places)


def shards(miller, form_factors, fractional, multipoles, point_owner, offsets):
    even_sign, odd_sign = sign_tables(form_factors.shape[0])
    phases = angles(miller, fractional)
    cos_table = jnp.cos(phases).astype(jnp.bfloat16)
    sin_table = jnp.sin(phases).astype(jnp.bfloat16)
    partial_sums = structure(multipoles, cos_table, sin_table, form_factors, even_sign, odd_sign)
    summed = lax.psum(partial_sums, "atoms")
    potential = coulomb(miller)[None, None, :] * summed
    local_moments = moment_terms(potential, form_factors, cos_table, sin_table, even_sign, odd_sign)
    moments = lax.psum_scatter(local_moments, "gsplit", scatter_dimension=2, tiled=True)
    atom_ids = jnp.arange(fractional.shape[1], dtype=jnp.int32)
    onehot = (atom_ids[:, None] == point_owner[None, :]).astype(jnp.float32)
    places = (
        jnp.dot(
            fractional, onehot, precision=lax.Precision.HIGHEST, preferred_element_type=jnp.float32
        )
        + offsets
    )
    rounded = potential.astype(jnp.bfloat16)
    every_vector = lax.all_gather(miller, "gsplit", axis=1, tiled=True)
    every_potential = lax.all_gather(rounded, "gsplit", axis=2, tiled=True)
    point_rows = grid_blocked(every_potential, every_vector, places)
    return (point_rows.T, moments)


def solution(mesh):
    placed = (
        P(None, "gsplit"),
        P(None, "gsplit"),
        P(None, "atoms"),
        P(None, None, "atoms"),
        P(("atoms", "gsplit")),
        P(None, ("atoms", "gsplit")),
    )
    return jax.shard_map(
        shards,
        mesh=mesh,
        in_specs=placed,
        out_specs=(P(None, ("atoms", "gsplit")), P(None, None, ("atoms", "gsplit"))),
        check_vma=False,
    )
```

profile of v0, /device:TPU:0, one launch (start us, length us, event | category | flops | bytes accessed | tf_op | source)
XLA Modules:
  0.0 180.9 jit_solution(15231726801209480579)
XLA Ops:
  7.2 0.0 all-reduce.3.cloned.1.call-start
  7.2 0.9 convert_element_type.435
  8.1 0.2 slice_reduce_fusion.2
  8.4 0.8 slice_bitcast_fusion.15
  9.2 0.8 copy.11
  10.0 0.1 reshape.154
  10.1 8.7 %convolution_bitcast_fusion.1 = f32[98,7680]{1,0:T(8,128)} fusion(bf16[98,64]{0,1:T(8,128)(2,1)S(1)} %reshape.154, f32[7680]{0:T(1024)S(1)} %get-tuple-element.11, f32[64]{0:T(128)S(1)} %get-tuple-element.20, f32[7680]{0:T(1024)S(1)} %get-tuple-element.12, f32[64]{0:T(128)S(1)} %get-tuple-element.19, f32[7680]{0:T(1024)S(1)} %get-tuple-element.10, ...), kind=kOutput, calls=%fused_computation.1 | convolution fusion | flops 99778560 | bytes 3116032 | tf_op jit(solution)/shard_map/dot_general | solution.py:41
  18.8 7.0 %convolution_bitcast_fusion = f32[98,7680]{1,0:T(8,128)S(1)} fusion(bf16[98,64]{0,1:T(8,128)(2,1)S(1)} %reshape.154, f32[7680]{0:T(1024)S(1)} %get-tuple-element.11, f32[64]{0:T(128)S(1)} %get-tuple-element.20, f32[7680]{0:T(1024)S(1)} %get-tuple-element.12, f32[64]{0:T(128)S(1)} %get-tuple-element.19, f32[7680]{0:T(1024)S(1)} %get-tuple-element.10, ...), kind=kOutput, calls=%fused_computation | convolution fusion | flops 99778560 | bytes 3116032 | tf_op jit(solution)/shard_map/dot_general | solution.py:44
  25.9 4.0 %reshape.155 = f32[2,49,7680]{2,1,0:T(8,128)} reshape(f32[98,7680]{1,0:T(8,128)} %convolution_bitcast_fusion.1) | data formatting | bytes 6021120 | tf_op jit(solution)/shard_map/reshape | solution.py:41
  29.8 2.1 %reshape.156 = f32[2,49,7680]{2,1,0:T(8,128)} reshape(f32[98,7680]{1,0:T(8,128)S(1)} %convolution_bitcast_fusion) | data formatting | bytes 6021120 | tf_op jit(solution)/shard_map/reshape | solution.py:44
  31.9 1.3 convert_element_type.436
  33.2 0.0 copy-start
  33.2 4.5 %multiply_reduce_fusion.1 = (f32[2,7680]{1,0:T(2,128)S(1)}, f32[2,7680]{1,0:T(2,128)S(1)}) fusion(f32[2,49,7680]{2,1,0:T(8,128)} %reshape.156, f32[2,49,7680]{2,1,0:T(8,128)} %reshape.155, f32[49]{0:T(128)S(1)} %get-tuple-element.24, f32[49]{0:T(128)S(1)} %get-tuple-element.25, f32[49,7680]{1,0:T(8,128)S(1)} %convert_element_type.436), kind=kLoop, calls=%fused_computation.7 | loop fusion | flops 7495680 | bytes 7649672 | tf_op jit(solution)/shard_map/reduce_sum | solution.py:50
  37.8 0.0 copy-start.4
  37.8 0.7 pad_maximum_fusion
  38.5 0.0 all-reduce.3.cloned.1.call-update
  38.6 17.6 %all_gather.7 = s32[3,30720]{1,0:T(4,128)S(1)} all-gather(s32[3,7680]{1,0:T(4,128)S(1)} %copy-done), channel_id=1, replica_groups=mesh['atoms'=8,'gsplit'=4] {'gsplit'}, dimensions={1}, use_global_device_ids=true | all-gather | bytes 460800 | tf_op jit(solution)/shard_map/all_gather | solution.py:113
  56.1 0.1 convert_element_type.455
  56.2 0.3 fusion.54
  56.5 0.1 fusion.8
  56.7 0.6 dynamic-slice
  57.9 36.2 %all-reduce.3.cloned.1.call-done = f32[2,2,7680]{2,0,1:T(2,128)} async-done(((f32[2,2,7680]{2,0,1:T(2,128)}), f32[2,2,7680]{2,0,1:T(2,128)}) %all-reduce.3.cloned.1.call-update) | async-done | bytes 122896 | tf_op jit(solution)/shard_map/psum | solution.py:100
  94.1 1.0 fusion.53
  95.1 0.4 multiply_convert_fusion
  95.5 7.4 %fusion.2 = f32[2,49,64]{2,1,0:T(8,128)S(1)} fusion(pred[49]{0:T(512)(128)(4,1)S(1)} %broadcast_compare_fusion, bf16[2,2,49,7680]{3,2,0,1:T(8,128)(2,1)S(1)} %multiply_convert_fusion, f32[7680]{0:T(1024)S(1)} %get-tuple-element.11, f32[64]{0:T(128)S(1)} %get-tuple-element.20, f32[7680]{0:T(1024)S(1)} %get-tuple-element.12, f32[64]{0:T(128)S(1)} %get-tuple-element.19, ...), kind=kOutput, calls=%fused_computation.15 | convolution fusion | flops 100531200 | bytes 3128625 | tf_op jit(solution)/shard_map/dot_general | solution.py:71
  102.9 7.5 %multiply_add_fusion = f32[2,49,64]{2,1,0:T(8,128)S(1)} fusion(f32[2,49,64]{2,1,0:T(8,128)S(1)} %fusion.2, f32[7680]{0:T(1024)S(1)} %get-tuple-element.11, f32[64]{0:T(128)S(1)} %get-tuple-element.20, f32[7680]{0:T(1024)S(1)} %get-tuple-element.12, f32[64]{0:T(128)S(1)} %get-tuple-element.19, f32[7680]{0:T(1024)S(1)} %get-tuple-element.10, ...), kind=kOutput, calls=%fused_computation.30 | convolution fusion | flops 100562560 | bytes 3154105 | tf_op jit(solution)/shard_map/dot_general | solution.py:68
  110.5 0.1 copy.12
  110.6 19.9 %all-reduce = f32[2,49,64]{1,0,2:T(2,128)S(1)} all-reduce(f32[2,49,64]{1,0,2:T(2,128)S(1)} %copy.12), channel_id=2, replica_groups=mesh['atoms'=8,'gsplit'=4] {'gsplit'}, use_global_device_ids=true, to_apply=%region_3.4.clone | all-reduce | flops 6272 | bytes 50176
  130.5 0.6 copy.13
  131.1 14.1 %all_gather.6 = bf16[2,2,30720]{2,0,1:T(2,128)(2,1)S(1)} all-gather(bf16[2,2,7680]{2,0,1:T(2,128)(2,1)S(1)} %get-tuple-element.13), channel_id=1, replica_groups=mesh['atoms'=8,'gsplit'=4] {'gsplit'}, dimensions={2}, use_global_device_ids=true | all-gather | bytes 307200 | tf_op jit(solution)/shard_map/all_gather | solution.py:114
  145.1 13.8 %fusion = f32[2,32]{1,0:T(2,128)S(1)} fusion(f32[30720]{0:T(1024)S(1)} %bitcast.69, f32[32]{0:T(128)S(1)} %get-tuple-element.22, f32[30720]{0:T(1024)S(1)} %bitcast.71, f32[32]{0:T(128)S(1)} %get-tuple-element.23, f32[30720]{0:T(1024)S(1)} %bitcast.67, f32[32]{0:T(128)S(1)} %get-tuple-element.21, bf16[2,2,30720]{2,0,1:T(2,128)(2,1)S(1)} %all_gather.6), kind=kOutput, calls=%fused_computation.11 | convolution fusion | flops 10813440 | bytes 493312 | tf_op jit(solution)/shard_map/dot_general | solution.py:84
  159.0 14.6 %fusion.9 = f32[2,32]{1,0:T(2,128)} fusion(f32[2,32]{1,0:T(2,128)S(1)} %fusion, f32[30720]{0:T(1024)S(1)} %bitcast.70, f32[32]{0:T(128)S(1)} %get-tuple-element.22, f32[30720]{0:T(1024)S(1)} %bitcast.72, f32[32]{0:T(128)S(1)} %get-tuple-element.23, f32[30720]{0:T(1024)S(1)} %bitcast.68, f32[32]{0:T(128)S(1)} %get-tuple-element.21, ...), kind=kOutput, calls=%fused_computation.23 | convolution fusion | flops 10813504 | bytes 494336 | tf_op jit(solution)/shard_map/dot_general | solution.py:86
  (13 shorter events, 0.1 us)
Async XLA Ops:
  7.2 87.0 %all-reduce.3.cloned.1.call-start = ((), (), s32[]{:S(2)}) async-start(), calls=%async_computation | async-start | bytes 245760 | tf_op jit(solution)/shard_map/psum | solution.py:100
  33.2 5.4 %copy-start = (s32[3,7680]{1,0:T(4,128)S(1)}, s32[3,7680]{1,0:T(4,128)}, u32[]{:S(2)}) copy-start(s32[3,7680]{1,0:T(4,128)} %param.6) | copy-start | bytes 276484
  37.7 18.7 %copy-start.1 = (f32[3,64]{1,0:T(4,128)S(1)}, f32[3,64]{1,0:T(4,128)}, u32[]{:S(2)}) copy-start(f32[3,64]{1,0:T(4,128)} %param.8) | copy-start | bytes 2308
  37.8 18.7 %copy-start.2 = (f32[3,32]{1,0:T(4,128)S(1)}, f32[3,32]{1,0:T(4,128)}, u32[]{:S(2)}) copy-start(f32[3,32]{1,0:T(4,128)} %param.11) | copy-start | bytes 1156
  37.8 18.7 %copy-start.3 = (s32[32]{0:T(128)S(1)}, s32[32]{0:T(128)}, u32[]{:S(2)}) copy-start(s32[32]{0:T(128)} %param.10) | copy-start | bytes 388
  37.8 18.9 %copy-start.4 = (u32[32]{0:T(128)S(1)}, u32[32]{0:T(128)}, u32[]{:S(2)}) copy-start(u32[32]{0:T(128)} %constant.62) | copy-start | bytes 388
Sparse Core Ops, SparseCore 0:
  38.6 55.4 all-reduce.2
where the time goes:
time: 184 us; the launch traced here: 181 us
  matrix products  59.2 us (32%)
  blocking collectives  51.5 us (28%)
  waiting for transfers between devices  36.2 us (20%)
  between operations  15.3 us (8%)
  local copies, waits for them, and re-layouts  9.62 us (5%)
  other arithmetic  8.97 us (5%)
    psum x1, waiting for transfers between devices, shards(): summed = lax.psum(partial_sums, 'atoms')  36.2 us
    unnamed x1, blocking collectives  19.9 us
    all_gather x1, blocking collectives, shards(): every_vector = lax.all_gather(miller, 'gsplit', axis=1, tiled=True)  17.6 us
    dot_general x1, matrix products, grid_rows(): lax.dot_general(sin_points, rounded[:, 1], contract, preferred_element_ty...  14.6 us
    all_gather x1, blocking collectives, shards(): every_potential = lax.all_gather(rounded, 'gsplit', axis=2, tiled=True)  14.1 us
    dot_general x1, matrix products, grid_rows(): lax.dot_general(cos_points, rounded[:, 0], contract, preferred_element_ty...  13.8 us
    dot_general x1, matrix products, structure(): jnp.dot(flattened, cos_table, preferred_element_type=jnp.float32)  8.67 us
    dot_general x1, matrix products, moment_terms(): lax.dot_general(against_cos, cos_table, contract, preferred_element_type=...  7.51 us
  transfers between devices with their start and end apart: 1, of which 1 were waited for; matrix products, arithmetic and copies ran while one was open for 1% of the time, Pallas kernels for 0%

commit v1 on v0

--- a/solution.py
+++ b/solution.py
@@ -111,7 +111,14 @@
     )
     rounded = potential.astype(jnp.bfloat16)
     every_vector = lax.all_gather(miller, "gsplit", axis=1, tiled=True)
-    every_potential = lax.all_gather(rounded, "gsplit", axis=2, tiled=True)
+    ring = [rounded]
+    for hop in range(3):
+        ring.append(lax.ppermute(ring[-1], "gsplit", [(dev, (dev + 1) % 4) for dev in range(4)]))
+    every_potential = jnp.roll(
+        jnp.concatenate(ring[::-1], axis=2),
+        (lax.axis_index("gsplit") + 1) * ring[0].shape[2],
+        axis=2,
+    )
     point_rows = grid_blocked(every_potential, every_vector, places)
     return (point_rows.T, moments)
 

time: 184 us -> 178 us (0.967)
  blocking collectives: 51.5 us -> 35.7 us
  waiting for transfers between devices: 36.2 us -> 42 us
  starting transfers between devices: 0.04 us -> 3.96 us
    all_gather x1 -> x0, blocking collectives: 14.1 us -> none  [shards(): every_potential = lax.all_gather(rounded, 'gsplit', axis=2, tiled=True)]
    ppermute x0 -> x3, waiting for transfers between devices: none -> 5.38 us  [shards(): lax.ppermute(ring[-1], 'gsplit', [(dev, (dev + 1) % 4) for dev in range(4)])]
    ppermute x0 -> x3, starting transfers between devices: none -> 3.92 us  [shards(): lax.ppermute(ring[-1], 'gsplit', [(dev, (dev + 1) % 4) for dev in range(4)])]
  transfers between devices with their start and end apart: 1 -> 4, of which waited for: 1 -> 2; matrix products, arithmetic and copies ran while one was open for 1% -> 9% of each run, Pallas kernels for 0% -> 0%
where the time goes in v1:
time: 178 us; the launch traced here: 175 us
  matrix products  59.2 us (33%)
  waiting for transfers between devices  42 us (24%)
  blocking collectives  35.7 us (20%)
  between operations  15.2 us (9%)
  local copies, waits for them, and re-layouts  10 us (6%)
  other arithmetic  8.97 us (5%)
  starting transfers between devices  3.96 us (2%)
    psum x1, waiting for transfers between devices, shards(): summed = lax.psum(partial_sums, 'atoms')  36.6 us
    unnamed x1, blocking collectives  18.6 us
    all_gather x1, blocking collectives, shards(): every_vector = lax.all_gather(miller, 'gsplit', axis=1, tiled=True)  17.1 us
    dot_general x1, matrix products, grid_rows(): lax.dot_general(cos_points, rounded[:, 0], contract, preferred_element_ty...  14.6 us
    dot_general x1, matrix products, grid_rows(): lax.dot_general(sin_points, rounded[:, 1], contract, preferred_element_ty...  14.1 us
    dot_general x1, matrix products, structure(): jnp.dot(flattened, cos_table, preferred_element_type=jnp.float32)  8.63 us
    dot_general x1, matrix products, moment_terms(): lax.dot_general(against_sin, sin_table, contract, preferred_element_type=...  7.4 us
    dot_general x1, matrix products, moment_terms(): lax.dot_general(against_cos, cos_table, contract, preferred_element_type=...  7.34 us
  transfers between devices with their start and end apart: 4, of which 2 were waited for; matrix products, arithmetic and copies ran while one was open for 9% of the time, Pallas kernels for 0%

profile of v1, /device:TPU:0, one launch (start us, length us, event | category | flops | bytes accessed | tf_op | source)
XLA Modules:
  0.0 175.1 jit_solution(6998674180137708004)
XLA Ops:
  7.2 0.9 convert_element_type.435
  8.1 0.2 slice_reduce_fusion.2
  8.4 0.8 slice_bitcast_fusion.11
  9.2 0.8 copy.11
  10.0 0.1 reshape.154
  10.1 8.6 %convolution_bitcast_fusion.1 = f32[98,7680]{1,0:T(8,128)} fusion(bf16[98,64]{0,1:T(8,128)(2,1)S(1)} %reshape.154, f32[7680]{0:T(1024)S(1)} %get-tuple-element.11, f32[64]{0:T(128)S(1)} %get-tuple-element.20, f32[7680]{0:T(1024)S(1)} %get-tuple-element.12, f32[64]{0:T(128)S(1)} %get-tuple-element.19, f32[7680]{0:T(1024)S(1)} %get-tuple-element.10, ...), kind=kOutput, calls=%fused_computation.1 | convolution fusion | flops 99778560 | bytes 3116032 | tf_op jit(solution)/shard_map/dot_general | solution.py:41
  18.8 7.0 %convolution_bitcast_fusion = f32[98,7680]{1,0:T(8,128)S(1)} fusion(bf16[98,64]{0,1:T(8,128)(2,1)S(1)} %reshape.154, f32[7680]{0:T(1024)S(1)} %get-tuple-element.11, f32[64]{0:T(128)S(1)} %get-tuple-element.20, f32[7680]{0:T(1024)S(1)} %get-tuple-element.12, f32[64]{0:T(128)S(1)} %get-tuple-element.19, f32[7680]{0:T(1024)S(1)} %get-tuple-element.10, ...), kind=kOutput, calls=%fused_computation | convolution fusion | flops 99778560 | bytes 3116032 | tf_op jit(solution)/shard_map/dot_general | solution.py:44
  25.8 4.0 %reshape.155 = f32[2,49,7680]{2,1,0:T(8,128)} reshape(f32[98,7680]{1,0:T(8,128)} %convolution_bitcast_fusion.1) | data formatting | bytes 6021120 | tf_op jit(solution)/shard_map/reshape | solution.py:41
  29.8 2.1 %reshape.156 = f32[2,49,7680]{2,1,0:T(8,128)} reshape(f32[98,7680]{1,0:T(8,128)S(1)} %convolution_bitcast_fusion) | data formatting | bytes 6021120 | tf_op jit(solution)/shard_map/reshape | solution.py:44
  31.9 1.3 convert_element_type.436
  33.2 4.5 %multiply_reduce_fusion.1 = (f32[2,7680]{1,0:T(2,128)S(1)}, f32[2,7680]{1,0:T(2,128)S(1)}) fusion(f32[2,49,7680]{2,1,0:T(8,128)} %reshape.156, f32[2,49,7680]{2,1,0:T(8,128)} %reshape.155, f32[49]{0:T(128)S(1)} %get-tuple-element.24, f32[49]{0:T(128)S(1)} %get-tuple-element.25, f32[49,7680]{1,0:T(8,128)S(1)} %convert_element_type.436), kind=kLoop, calls=%fused_computation.7 | loop fusion | flops 7495680 | bytes 7649672 | tf_op jit(solution)/shard_map/reduce_sum | solution.py:50
  37.7 0.7 pad_maximum_fusion
  38.5 17.1 %all_gather.3 = s32[3,30720]{1,0:T(4,128)S(1)} all-gather(s32[3,7680]{1,0:T(4,128)S(1)} %copy-done), channel_id=1, replica_groups=mesh['atoms'=8,'gsplit'=4] {'gsplit'}, dimensions={1}, use_global_device_ids=true | all-gather | bytes 460800 | tf_op jit(solution)/shard_map/all_gather | solution.py:113
  55.6 0.1 convert_element_type.455
  55.7 0.3 fusion.56
  56.0 0.1 fusion.8
  56.2 0.6 dynamic-slice
  57.4 36.6 %all-reduce.3.cloned.1.call-done = f32[2,2,7680]{2,0,1:T(2,128)} async-done(((f32[2,2,7680]{2,0,1:T(2,128)}), f32[2,2,7680]{2,0,1:T(2,128)}) %all-reduce.3.cloned.1.call-update) | async-done | bytes 122896 | tf_op jit(solution)/shard_map/psum | solution.py:100
  94.1 1.0 fusion.55
  95.1 0.4 multiply_convert_fusion
  95.5 1.8 collective-permute-start
  97.2 7.4 %fusion.2 = f32[2,49,64]{2,1,0:T(8,128)S(1)} fusion(pred[49]{0:T(512)(128)(4,1)S(1)} %broadcast_compare_fusion, bf16[2,2,49,7680]{3,2,0,1:T(8,128)(2,1)S(1)} %multiply_convert_fusion, f32[7680]{0:T(1024)S(1)} %get-tuple-element.11, f32[64]{0:T(128)S(1)} %get-tuple-element.20, f32[7680]{0:T(1024)S(1)} %get-tuple-element.12, f32[64]{0:T(128)S(1)} %get-tuple-element.19, ...), kind=kOutput, calls=%fused_computation.15 | convolution fusion | flops 100531200 | bytes 3128625 | tf_op jit(solution)/shard_map/dot_general | solution.py:71
  104.6 1.9 %collective-permute-start.1 = (bf16[2,2,7680]{2,0,1:T(2,128)(2,1)S(1)}, bf16[2,2,7680]{2,0,1:T(2,128)(2,1)S(1)}, u32[]{:S(2)}, u32[]{:S(2)}) collective-permute-start(bf16[2,2,7680]{2,0,1:T(2,128)(2,1)S(1)} %collective-permute-done), channel_id=1, source_target_pairs={{0,1},{1,2},{2,3},{3,0},{4,5},{5,6},{6,7},{7,4},{8,9},{9,10},{10,1... | collective-permute-start | bytes 184328 | tf_op jit(solution)/shard_map/ppermute | solution.py:116
  106.6 7.3 %multiply_add_fusion = f32[2,49,64]{2,1,0:T(8,128)S(1)} fusion(f32[2,49,64]{2,1,0:T(8,128)S(1)} %fusion.2, f32[7680]{0:T(1024)S(1)} %get-tuple-element.11, f32[64]{0:T(128)S(1)} %get-tuple-element.20, f32[7680]{0:T(1024)S(1)} %get-tuple-element.12, f32[64]{0:T(128)S(1)} %get-tuple-element.19, f32[7680]{0:T(1024)S(1)} %get-tuple-element.10, ...), kind=kOutput, calls=%fused_computation.30 | convolution fusion | flops 100562560 | bytes 3154105 | tf_op jit(solution)/shard_map/dot_general | solution.py:68
  113.9 0.1 copy.12
  114.0 18.6 %all-reduce = f32[2,49,64]{1,0,2:T(2,128)S(1)} all-reduce(f32[2,49,64]{1,0,2:T(2,128)S(1)} %copy.12), channel_id=2, replica_groups=mesh['atoms'=8,'gsplit'=4] {'gsplit'}, use_global_device_ids=true, to_apply=%region_3.4.clone | all-reduce | flops 6272 | bytes 50176
  132.7 0.2 collective-permute-start.2
  132.9 0.6 copy.13
  133.6 5.4 %collective-permute-done.2 = bf16[2,2,7680]{2,0,1:T(2,128)(2,1)S(1)} collective-permute-done((bf16[2,2,7680]{2,0,1:T(2,128)(2,1)S(1)}, bf16[2,2,7680]{2,0,1:T(2,128)(2,1)S(1)}, u32[]{:S(2)}, u32[]{:S(2)}) %collective-permute-start.2) | collective-permute-done | bytes 61472 | tf_op jit(solution)/shard_map/ppermute | solution.py:116
  139.2 0.1 constant_dynamic-update-slice_fusion.3
  139.4 14.1 %fusion.1 = f32[2,32]{1,0:T(2,128)S(1)} fusion(f32[30720]{0:T(1024)S(1)} %bitcast.69, f32[32]{0:T(128)S(1)} %get-tuple-element.22, f32[30720]{0:T(1024)S(1)} %bitcast.71, f32[32]{0:T(128)S(1)} %get-tuple-element.23, f32[30720]{0:T(1024)S(1)} %bitcast.67, f32[32]{0:T(128)S(1)} %get-tuple-element.21, ...), kind=kOutput, calls=%fused_computation.12 | convolution fusion | flops 10813440 | bytes 493320 | tf_op jit(solution)/shard_map/dot_general | solution.py:86
  153.5 14.6 %fusion.9 = f32[2,32]{1,0:T(2,128)} fusion(f32[2,32]{1,0:T(2,128)S(1)} %fusion.1, f32[30720]{0:T(1024)S(1)} %bitcast.70, f32[32]{0:T(128)S(1)} %get-tuple-element.22, f32[30720]{0:T(1024)S(1)} %bitcast.72, f32[32]{0:T(128)S(1)} %get-tuple-element.23, f32[30720]{0:T(1024)S(1)} %bitcast.68, f32[32]{0:T(128)S(1)} %get-tuple-element.21, ...), kind=kOutput, calls=%fused_computation.23 | convolution fusion | flops 10813504 | bytes 494340 | tf_op jit(solution)/shard_map/dot_general | solution.py:84
  (26 shorter events, 0.6 us)
Async XLA Ops:
  7.2 86.9 %all-reduce.3.cloned.1.call-start = ((), (), s32[]{:S(2)}) async-start(), calls=%async_computation | async-start | bytes 245760 | tf_op jit(solution)/shard_map/psum | solution.py:100
  33.1 5.4 %copy-start = (s32[3,7680]{1,0:T(4,128)S(1)}, s32[3,7680]{1,0:T(4,128)}, u32[]{:S(2)}) copy-start(s32[3,7680]{1,0:T(4,128)} %param.6) | copy-start | bytes 276484
  37.7 18.3 %copy-start.1 = (f32[3,64]{1,0:T(4,128)S(1)}, f32[3,64]{1,0:T(4,128)}, u32[]{:S(2)}) copy-start(f32[3,64]{1,0:T(4,128)} %param.8) | copy-start | bytes 2308
  37.7 18.3 %copy-start.2 = (f32[3,32]{1,0:T(4,128)S(1)}, f32[3,32]{1,0:T(4,128)}, u32[]{:S(2)}) copy-start(f32[3,32]{1,0:T(4,128)} %param.11) | copy-start | bytes 1156
  37.7 18.3 %copy-start.3 = (s32[32]{0:T(128)S(1)}, s32[32]{0:T(128)}, u32[]{:S(2)}) copy-start(s32[32]{0:T(128)} %param.10) | copy-start | bytes 388
  37.7 18.4 %copy-start.4 = (u32[32]{0:T(128)S(1)}, u32[32]{0:T(128)}, u32[]{:S(2)}) copy-start(u32[32]{0:T(128)} %constant.87) | copy-start | bytes 388
  95.5 9.2 %collective-permute-start = (bf16[2,2,7680]{2,0,1:T(2,128)(2,1)S(1)}, bf16[2,2,7680]{2,0,1:T(2,128)(2,1)S(1)}, u32[]{:S(2)}, u32[]{:S(2)}) collective-permute-start(bf16[2,2,7680]{2,0,1:T(2,128)(2,1)S(1)} %get-tuple-element.13), channel_id=1, source_target_pairs={{0,1},{1,2},{2,3},{3,0},{4,5},{5,6},{6,7},{7,4},{8,9},{9,10},{10,1... | collective-permute-start | bytes 184328 | tf_op jit(solution)/shard_map/ppermute | solution.py:116
  104.6 28.0 %collective-permute-start.1 = (bf16[2,2,7680]{2,0,1:T(2,128)(2,1)S(1)}, bf16[2,2,7680]{2,0,1:T(2,128)(2,1)S(1)}, u32[]{:S(2)}, u32[]{:S(2)}) collective-permute-start(bf16[2,2,7680]{2,0,1:T(2,128)(2,1)S(1)} %collective-permute-done), channel_id=1, source_target_pairs={{0,1},{1,2},{2,3},{3,0},{4,5},{5,6},{6,7},{7,4},{8,9},{9,10},{10,1... | collective-permute-start | bytes 184328 | tf_op jit(solution)/shard_map/ppermute | solution.py:116
  132.7 6.2 %collective-permute-start.2 = (bf16[2,2,7680]{2,0,1:T(2,128)(2,1)S(1)}, bf16[2,2,7680]{2,0,1:T(2,128)(2,1)S(1)}, u32[]{:S(2)}, u32[]{:S(2)}) collective-permute-start(bf16[2,2,7680]{2,0,1:T(2,128)(2,1)S(1)} %collective-permute-done.1), channel_id=1, source_target_pairs={{0,1},{1,2},{2,3},{3,0},{4,5},{5,6},{6,7},{7,4},{8,9},{9,10},{10,1... | collective-permute-start | bytes 184328 | tf_op jit(solution)/shard_map/ppermute | solution.py:116
Sparse Core Ops, SparseCore 0:
  38.6 55.4 all-reduce.2
